TPU v7x, 32 devices: a whole 2x2x4 slice. The times are simulated.
32 devices in a mesh: groups: 2 (over y), seq: 16 (over z, x, core).
Axes of the slice: x: 2, y: 2, z: 4, core: 2. Of those that a mesh axis runs over, the one named last changes fastest.
Arguments:
- query_rows: bfloat16 [2048, 2048], P(('groups', 'seq')), parts along dimension 0, may hold values from -180 to 180
- key_rows: bfloat16 [2048, 512], P(('groups', 'seq')), parts along dimension 0, may hold values from -6 to 6
- value_rows: bfloat16 [2048, 512], P(('groups', 'seq')), parts along dimension 0, may hold values from -6 to 6
- positions: int32 [2048], P(('groups', 'seq')), parts along dimension 0, may hold values from 0 to 1023, as said below
- prompt_length: int32 [2], P('groups'), parts along dimension 0, may hold values from 512 to 1024
- out_weight: bfloat16 [2048, 2048], replicated, may hold values from -0.125 to 0.125
- residual: bfloat16 [2048, 2048], P(('groups', 'seq')), parts along dimension 0, may hold values from -0.59765625 to 0.59765625
Outputs:
- layer_out: bfloat16 [2048, 2048], P(('groups', 'seq')), parts along dimension 0
There are 2 independent parts, one for each index of `groups`. A program takes and returns all parts, laid end to end along the dimension named above; an argument that names none is the same for every part. Nothing has to cross between parts.
Inputs may be any that keep to these rules, and one draw needn't show every extreme that they name: A permutation of 0 to 1023 in which each device's rows hold exactly one position of every run of 16 consecutive positions.
All inputs are finite; a program needn't handle non-finite values.
Results may differ from a plain program's by a relative error of at most 0.009.
Values may be sent and summed in bfloat16 or wider, within the bound.
A program may use at most 128 MiB of HBM per device.

v0:
```python
import jax
import jax.numpy as jnp
from jax import lax
from jax.sharding import PartitionSpec as P

HEADS = 16
KV_HEADS = 4
HEAD_DIM = 128


def largest_block(total_rows):
    size_now = min(total_rows, 1024)
    while total_rows % size_now:
        size_now -= 1
    return size_now


def attend_block(state_now, key_part, value_part, key_pos, queries, query_pos, prompt_limit):
    maxima, totals, numerators = state_now
    scores = jnp.einsum(
        "hqd,khd->hqk", queries, key_part, preferred_element_type=jnp.float32
    ) * HEAD_DIM ** (-0.5)
    visible = (key_pos[None, None, :] <= query_pos[None, :, None]) & (
        key_pos[None, None, :] < prompt_limit
    )
    scores = jnp.where(visible, scores, -1e30)
    new_max = jnp.maximum(maxima, jnp.max(scores, axis=-1))
    weights = jnp.where(visible, jnp.exp(scores - new_max[..., None]), 0.0)
    rescale = jnp.exp(maxima - new_max)
    totals = totals * rescale + jnp.sum(weights, axis=-1)
    numerators = numerators * rescale[..., None] + jnp.einsum(
        "hqk,khd->hqd", weights.astype(jnp.bfloat16), value_part, preferred_element_type=jnp.float32
    )
    return (new_max, totals, numerators)


def sweep(state_now, key_block, value_block, key_pos, queries, query_pos, prompt_limit):
    total_rows = key_block.shape[0]
    width_rows = largest_block(total_rows)
    key_part = key_block.reshape(total_rows, KV_HEADS, HEAD_DIM)
    value_part = value_block.reshape(total_rows, KV_HEADS, HEAD_DIM)
    if width_rows == total_rows:
        return attend_block(
            state_now, key_part, value_part, key_pos, queries, query_pos, prompt_limit
        )
    count_blocks = total_rows // width_rows
    stacked = (
        key_part.reshape(count_blocks, width_rows, KV_HEADS, HEAD_DIM),
        value_part.reshape(count_blocks, width_rows, KV_HEADS, HEAD_DIM),
        key_pos.reshape(count_blocks, width_rows),
    )

    def step_block(state_in, blocks):
        return (
            attend_block(
                state_in, blocks[0], blocks[1], blocks[2], queries, query_pos, prompt_limit
            ),
            None,
        )

    state_out, unused = lax.scan(step_block, state_now, stacked)
    return state_out


def on_device(query_rows, key_rows, value_rows, positions, prompt_length, out_weight, residual):
    tokens_here = query_rows.shape[0]
    group_size = HEADS // KV_HEADS
    queries = query_rows.reshape(tokens_here, KV_HEADS, group_size, HEAD_DIM).transpose(1, 2, 0, 3)
    queries = queries.reshape(KV_HEADS, group_size * tokens_here, HEAD_DIM)
    query_pos = jnp.tile(positions, group_size)
    prompt_limit = prompt_length[0]
    start_state = (
        jnp.full((KV_HEADS, group_size * tokens_here), -1e30, jnp.float32),
        jnp.zeros((KV_HEADS, group_size * tokens_here), jnp.float32),
        jnp.zeros((KV_HEADS, group_size * tokens_here, HEAD_DIM), jnp.float32),
    )
    final_state = sweep(
        start_state,
        lax.all_gather(key_rows, "seq", axis=0, tiled=True),
        lax.all_gather(value_rows, "seq", axis=0, tiled=True),
        lax.all_gather(positions, "seq", axis=0, tiled=True),
        queries,
        query_pos,
        prompt_limit,
    )
    maxima, totals, numerators = final_state
    attended = (numerators / totals[..., None]).reshape(KV_HEADS, group_size, tokens_here, HEAD_DIM)
    attended = (
        attended.transpose(2, 0, 1, 3).reshape(tokens_here, HEADS * HEAD_DIM).astype(jnp.bfloat16)
    )
    projected = jnp.dot(attended, out_weight, preferred_element_type=jnp.float32)
    return (projected + residual.astype(jnp.float32)).astype(jnp.bfloat16)


def solution(mesh):
    return jax.shard_map(
        on_device,
        mesh=mesh,
        in_specs=(
            P(("groups", "seq"), None),
            P(("groups", "seq"), None),
            P(("groups", "seq"), None),
            P(("groups", "seq")),
            P("groups"),
            P(),
            P(("groups", "seq"), None),
        ),
        out_specs=P(("groups", "seq"), None),
        check_vma=False,
    )
```

profile of v0, /device:TPU:0, one launch (start us, length us, event | category | flops | bytes accessed | tf_op | source)
XLA Modules:
  0.0 107.2 jit_solution(2775416098003896786)
XLA Ops:
  6.5 0.0 all-gather.3.cloned.1.call-start
  6.5 0.7 all-gather.3.cloned.1.call-update
  7.3 0.0 all-gather.5.cloned.1.call-start
  7.3 0.7 all-gather.5.cloned.1.call-update
  8.7 0.7 tile.2
  9.3 0.1 le.21
  9.4 1.1 %reshape.85 = bf16[64,4,4,128]{3,2,1,0:T(4,128)(2,1)S(1)} reshape(bf16[64,2048]{1,0:T(8,128)(2,1)} %param.7) | data formatting | bytes 524288 | tf_op jit(solution)/shard_map/reshape | solution.py:68
  10.5 0.1 copy.15
  10.6 1.2 %dynamic-slice = u32[1]{0:T(128)} dynamic-slice(u32[32]{0:T(128)} %constant.14, u32[]{:T(128)S(6)} %add.16), dynamic_slice_sizes={1} | dynamic-slice | bytes 12
  12.5 0.9 dynamic-update-slice
  13.4 13.8 %all-reduce = s32[1024]{0:T(1024)S(1)} all-reduce(s32[1024]{0:T(1024)S(1)} %dynamic-update-slice), channel_id=1, replica_groups=mesh['groups'=2,'seq'=16] {'seq'}, use_global_device_ids=true, to_apply=%add | all-reduce | flops 1024 | bytes 8192
  27.2 0.2 compare_and_fusion
  27.4 22.7 %all-gather.3.cloned.1.call-done = bf16[1024,512]{1,0:T(8,128)(2,1)} async-done(((bf16[64,512]{1,0:T(8,128)(2,1)}), bf16[1024,512]{1,0:T(8,128)(2,1)}) %all-gather.3.cloned.1.call-update) | async-done | bytes 1048592 | tf_op jit(solution)/shard_map/all_gather | solution.py:79
  50.1 1.5 %copy.16 = bf16[1024,512]{0,1:T(8,128)(2,1)S(1)} copy(bf16[1024,512]{1,0:T(8,128)(2,1)} %all-gather.3.cloned.1.call-done) | data formatting | bytes 2097152 | tf_op jit(solution)/shard_map/all_gather | solution.py:79
  51.6 1.0 fusion
  52.6 1.9 %copy-done = f32[4,256,1024]{2,1,0:T(8,128)} copy-done((f32[4,256,1024]{2,1,0:T(8,128)}, f32[4,256,1024]{2,1,0:T(8,128)S(1)}, u32[]{:S(2)}) %copy-start) | copy-done | bytes 4194328
  54.6 1.5 %fusion.1 = f32[4,256]{1,0:T(4,128)S(1)} fusion(f32[4,256,1024]{2,1,0:T(8,128)S(1)} %get-tuple-element.8, f32[4,256]{1,0:T(4,128)S(1)} %broadcast_maximum_fusion, pred[256,1024]{1,0:T(8,128)(4,1)S(1)} %compare_and_fusion), kind=kLoop, calls=%fused_computation.3 | loop fusion | flops 5241856 | bytes 4464640 | tf_op jit(solution)/shard_map/reduce_sum | solution.py:30
  56.1 33.0 %all-gather.5.cloned.1.call-done = bf16[1024,512]{1,0:T(8,128)(2,1)} async-done(((bf16[64,512]{1,0:T(8,128)(2,1)}), bf16[1024,512]{1,0:T(8,128)(2,1)}) %all-gather.5.cloned.1.call-update) | async-done | bytes 1048592 | tf_op jit(solution)/shard_map/all_gather | solution.py:80
  89.1 1.5 %copy.18 = bf16[1024,512]{0,1:T(8,128)(2,1)S(1)} copy(bf16[1024,512]{1,0:T(8,128)(2,1)} %all-gather.5.cloned.1.call-done) | data formatting | bytes 2097152 | tf_op jit(solution)/shard_map/all_gather | solution.py:80
  90.6 0.0 copy-start.1
  90.6 3.7 %fusion.13 = bf16[4,256,128]{2,1,0:T(8,128)(2,1)S(1)} fusion(bf16[1024,4,128]{0,2,1:T(8,128)(2,1)S(1)} %bitcast.18, f32[4,256,1024]{2,1,0:T(8,128)} %copy-done, f32[4,256]{1,0:T(4,128)S(1)} %broadcast_maximum_fusion, pred[256,1024]{1,0:T(8,128)(4,1)S(1)} %compare_and_fusion, f32[4,256]{1,0:T(4,128)S(1)} %get-tuple-element.6, f32[4,256]{1,0:T(4,128)S(1)} %get-tuple-element.5), kind=kOutput, calls=%fused_computation.12 | convolution fusion | flops 274071552 | bytes 5779456 | tf_op jit(solution)/shard_map/hqk,khd->hqd/dot_general | solution.py:31
  94.3 0.2 copy.24
  94.5 0.2 convert_element_type.25
  94.7 5.7 %fusion.3 = bf16[64,2048]{1,0:T(8,128)(2,1)} fusion(bf16[64,2048]{1,0:T(8,128)(2,1)S(1)} %convert_element_type.25, bf16[2048,2048]{1,0:T(8,128)(2,1)} %param.12, bf16[64,2048]{1,0:T(8,128)(2,1)S(1)} %copy-done.1), kind=kOutput, calls=%fused_computation.6 | convolution fusion | flops 537264128 | bytes 9175040 | tf_op jit(solution)/shard_map/dot_general | solution.py:91
  (6 shorter events, 0.0 us)
Async XLA Ops:
  6.5 43.6 %all-gather.3.cloned.1.call-start = ((), (), s32[]{:S(2)}) async-start(), calls=%async_computation | async-start | bytes 1114112 | tf_op jit(solution)/shard_map/all_gather | solution.py:79
  7.3 81.9 %all-gather.5.cloned.1.call-start = ((), (), s32[]{:S(2)}) async-start(), calls=%async_computation.1 | async-start | bytes 1114112 | tf_op jit(solution)/shard_map/all_gather | solution.py:80
  52.6 1.9 %copy-start = (f32[4,256,1024]{2,1,0:T(8,128)}, f32[4,256,1024]{2,1,0:T(8,128)S(1)}, u32[]{:S(2)}) copy-start(f32[4,256,1024]{2,1,0:T(8,128)S(1)} %get-tuple-element.8) | copy-start | bytes 12582916
  90.6 4.1 %copy-start.1 = (bf16[64,2048]{1,0:T(8,128)(2,1)S(1)}, bf16[64,2048]{1,0:T(8,128)(2,1)}, u32[]{:S(2)}) copy-start(bf16[64,2048]{1,0:T(8,128)(2,1)} %param.13) | copy-start | bytes 786436
Sparse Core Ops, SparseCore 0:
  9.5 40.5 all-gather.2
  52.3 36.8 all-gather.4
where the time goes:
time: 108 us; the launch traced here: 107 us
  waiting for transfers between devices  57.1 us (53%)
  between operations  14.8 us (14%)
  blocking collectives  13.8 us (13%)
  matrix products  10.4 us (10%)
  local copies, waits for them, and re-layouts  9.31 us (9%)
  other arithmetic  1.79 us (2%)
    all_gather x1, waiting for transfers between devices, on_device(): lax.all_gather(value_rows, 'seq', axis=0, tiled=True)  33 us
    all_gather x1, waiting for transfers between devices, on_device(): lax.all_gather(key_rows, 'seq', axis=0, tiled=True)  22.7 us
    unnamed x1, blocking collectives  13.8 us
    dot_general x1, matrix products, on_device(): jnp.dot(attended, out_weight, preferred_element_type=jnp.float32)  5.66 us
    unnamed x7, local copies, waits for them, and re-layouts  4.04 us
    dot_general x1, matrix products, attend_block(): jnp.einsum('hqk,khd->hqd', weights.astype(jnp.bfloat16), value_part, pref...  3.7 us
  transfers between devices with their start and end apart: 2, of which 2 were waited for; matrix products, arithmetic and copies ran while one was open for 8% of the time, Pallas kernels for 0%

commit v1 on v0

--- a/solution.py
+++ b/solution.py
@@ -1,11 +1,234 @@
+import functools
+import math
+
 import jax
 import jax.numpy as jnp
 from jax import lax
+from jax.experimental import pallas as pl
+from jax.experimental.pallas import tpu as pltpu
 from jax.sharding import PartitionSpec as P
 
+HEAD_DIM = 128
 HEADS = 16
 KV_HEADS = 4
-HEAD_DIM = 128
+UNROLLED_DEVICES = 32
+
+
+def split_chips(seq):
+    chips = seq // 2
+    x_size = 1
+    while 2 * x_size * 2 * x_size <= chips:
+        x_size *= 2
+    return x_size, chips // x_size
+
+
+def fused_kernel(
+    seq, x_size, z_size, kv_heads,
+    limit_ref, pos_ref, query_hbm, key_hbm, value_hbm, weight_hbm, residual_hbm,
+    out_ref,
+    kv, pos_all, query, weight, residual, bias, acc,
+    load_sem, kv_sem, weight_sem, send_sem, recv_sem, pos_send, pos_recv,
+):
+    tokens = query.shape[0]
+    group = query.shape[1] // (kv_heads * HEAD_DIM)
+    feat = group * HEAD_DIM
+    keys = seq * tokens
+    me = lax.axis_index("seq")
+    core = lax.rem(me, 2)
+    x_at = lax.rem(me // 2, x_size)
+    z_at = me // (2 * x_size)
+
+    def index_of(z, x, c):
+        return (z * x_size + x) * 2 + c
+
+    z_peers = [index_of(lax.rem(z_at + d, z_size), x_at, core) for d in range(1, z_size)]
+    x_ids = [lax.rem(x_at + d, x_size) for d in range(1, x_size)]
+    x_peers = [index_of(z_at, x, core) for x in x_ids]
+    other = index_of(z_at, x_at, 1 - core)
+    peers = z_peers + x_peers + [other]
+
+    local = []
+    for g in range(kv_heads):
+        cols = pl.ds(g * HEAD_DIM, HEAD_DIM)
+        pair = [
+            pltpu.make_async_copy(key_hbm.at[:, cols], kv.at[g, me, 0], kv_sem.at[g, 0]),
+            pltpu.make_async_copy(value_hbm.at[:, cols], kv.at[g, me, 1], kv_sem.at[g, 1]),
+        ]
+        for copy in pair:
+            copy.start()
+        local.append(pair)
+
+    barrier = pltpu.get_barrier_semaphore()
+    for peer in peers:
+        pl.semaphore_signal(
+            barrier, inc=1, device_id={"seq": peer}, device_id_type=pl.DeviceIdType.MESH
+        )
+    load_q = pltpu.make_async_copy(query_hbm, query, load_sem.at[0])
+    load_r = pltpu.make_async_copy(residual_hbm, residual, load_sem.at[1])
+    load_q.start()
+    load_r.start()
+    load_w = []
+    for g in range(kv_heads):
+        rows = pl.ds(g * feat, feat)
+        copy = pltpu.make_async_copy(weight_hbm.at[rows], weight.at[rows], weight_sem.at[g])
+        copy.start()
+        load_w.append(copy)
+    pl.semaphore_wait(barrier, len(peers))
+
+    sends = []
+    counts = [0] * kv_heads
+
+    def send(g, slot, peer):
+        if g == 0:
+            copy = pltpu.make_async_remote_copy(
+                src_ref=pos_all.at[slot], dst_ref=pos_all.at[slot],
+                send_sem=pos_send.at[counts[g]], recv_sem=pos_recv.at[slot],
+                device_id={"seq": peer}, device_id_type=pl.DeviceIdType.MESH,
+            ) if slot is not me else pltpu.make_async_remote_copy(
+                src_ref=pos_ref, dst_ref=pos_all.at[slot],
+                send_sem=pos_send.at[counts[g]], recv_sem=pos_recv.at[slot],
+                device_id={"seq": peer}, device_id_type=pl.DeviceIdType.MESH,
+            )
+            copy.start()
+            sends.append(copy)
+        copy = pltpu.make_async_remote_copy(
+            src_ref=kv.at[g, slot], dst_ref=kv.at[g, slot],
+            send_sem=send_sem.at[g, counts[g]], recv_sem=recv_sem.at[g, slot],
+            device_id={"seq": peer}, device_id_type=pl.DeviceIdType.MESH,
+        )
+        copy.start()
+        sends.append(copy)
+        counts[g] += 1
+
+    def arrive(g, slot):
+        if g == 0:
+            pltpu.make_async_remote_copy(
+                src_ref=pos_all.at[slot], dst_ref=pos_all.at[slot],
+                send_sem=pos_send.at[0], recv_sem=pos_recv.at[slot],
+                device_id={"seq": other}, device_id_type=pl.DeviceIdType.MESH,
+            ).wait_recv()
+        pltpu.make_async_remote_copy(
+            src_ref=kv.at[g, slot], dst_ref=kv.at[g, slot],
+            send_sem=send_sem.at[g, 0], recv_sem=recv_sem.at[g, slot],
+            device_id={"seq": other}, device_id_type=pl.DeviceIdType.MESH,
+        ).wait_recv()
+
+    z_slots = z_peers
+    x_slots = [
+        index_of(lax.rem(z_at + d, z_size), x, core) for d in range(z_size) for x in x_ids
+    ]
+    d_slots = [other]
+    d_slots += [index_of(lax.rem(z_at + d, z_size), x_at, 1 - core) for d in range(1, z_size)]
+    d_slots += [
+        index_of(lax.rem(z_at + d, z_size), x, 1 - core) for d in range(z_size) for x in x_ids
+    ]
+
+    for g in range(kv_heads):
+        for copy in local[g]:
+            copy.wait()
+        for peer in z_peers + x_peers + [other]:
+            send(g, me, peer)
+
+    def forward_z(g):
+        for slot in z_slots:
+            arrive(g, slot)
+            for peer in x_peers:
+                send(g, slot, peer)
+            send(g, slot, other)
+
+    def forward_x(g):
+        for slot in x_slots:
+            arrive(g, slot)
+            send(g, slot, other)
+
+    def receive(g):
+        for slot in d_slots:
+            arrive(g, slot)
+
+    def make_bias():
+        own = pos_ref[...]
+        pos_all[me] = own
+        square = jnp.broadcast_to(own, (tokens, tokens))
+        diag = lax.broadcasted_iota(jnp.int32, (tokens, tokens), 0) == (
+            lax.broadcasted_iota(jnp.int32, (tokens, tokens), 1)
+        )
+        column = jnp.sum(jnp.where(diag, square, 0), axis=1, keepdims=True)
+        cut = jnp.minimum(column, limit_ref[0] - 1)
+        row = jnp.concatenate([pos_all[s] for s in range(seq)], axis=1)
+        bias[...] = jnp.where(row <= cut, 0.0, -1e30)
+
+    def compute(g):
+        q = jnp.concatenate(
+            [query[:, (g * group + i) * HEAD_DIM:(g * group + i + 1) * HEAD_DIM] for i in range(group)],
+            axis=0,
+        )
+        k = kv[g, :, 0].reshape(keys, HEAD_DIM)
+        v = kv[g, :, 1].reshape(keys, HEAD_DIM)
+        s = lax.dot_general(q, k, (((1,), (1,)), ((), ())), preferred_element_type=jnp.float32)
+        s = s.reshape(group, tokens, keys) * (HEAD_DIM ** -0.5 * math.log2(math.e)) + bias[...][None]
+        s = s.reshape(group * tokens, keys)
+        p = jnp.exp2(s - jnp.max(s, axis=1, keepdims=True))
+        total = jnp.sum(p, axis=1, keepdims=True)
+        o = jnp.dot(p.astype(jnp.bfloat16), v, preferred_element_type=jnp.float32)
+        o = (o / total).astype(jnp.bfloat16)
+        a = jnp.concatenate([o[i * tokens:(i + 1) * tokens] for i in range(group)], axis=1)
+        load_w[g].wait()
+        part = jnp.dot(a, weight[g * feat:(g + 1) * feat, :], preferred_element_type=jnp.float32)
+        if g == 0:
+            load_r.wait()
+            acc[...] = part + residual[...].astype(jnp.float32)
+        elif g < kv_heads - 1:
+            acc[...] += part
+        else:
+            out_ref[...] = (acc[...] + part).astype(jnp.bfloat16)
+
+    forward_z(0)
+    load_q.wait()
+    for g in range(kv_heads):
+        if g + 1 < kv_heads:
+            forward_z(g + 1)
+        forward_x(g)
+        receive(g)
+        if g == 0:
+            make_bias()
+        if g == kv_heads - 1:
+            for copy in sends:
+                copy.wait_send()
+        compute(g)
+
+
+def fused(seq, query_rows, key_rows, value_rows, positions, prompt_length, out_weight, residual):
+    x_size, z_size = split_chips(seq)
+    tokens = query_rows.shape[0]
+    kv_heads = key_rows.shape[1] // HEAD_DIM
+    steps = (z_size - 1) * (x_size + 1) + x_size + (x_size - 1) * z_size
+    hbm = pl.BlockSpec(memory_space=pl.ANY)
+    vmem = pl.BlockSpec(memory_space=pltpu.VMEM)
+    return pl.pallas_call(
+        functools.partial(fused_kernel, seq, x_size, z_size, kv_heads),
+        out_shape=jax.ShapeDtypeStruct(residual.shape, jnp.bfloat16),
+        in_specs=[pl.BlockSpec(memory_space=pltpu.SMEM), vmem, hbm, hbm, hbm, hbm, hbm],
+        out_specs=vmem,
+        scratch_shapes=[
+            pltpu.VMEM((kv_heads, seq, 2, tokens, HEAD_DIM), jnp.bfloat16),
+            pltpu.VMEM((seq, 1, tokens), jnp.int32),
+            pltpu.VMEM(query_rows.shape, jnp.bfloat16),
+            pltpu.VMEM(out_weight.shape, jnp.bfloat16),
+            pltpu.VMEM(residual.shape, jnp.bfloat16),
+            pltpu.VMEM((tokens, seq * tokens), jnp.float32),
+            pltpu.VMEM(residual.shape, jnp.float32),
+            pltpu.SemaphoreType.DMA((2,)),
+            pltpu.SemaphoreType.DMA((kv_heads, 2)),
+            pltpu.SemaphoreType.DMA((kv_heads,)),
+            pltpu.SemaphoreType.DMA((kv_heads, steps + z_size)),
+            pltpu.SemaphoreType.DMA((kv_heads, seq)),
+            pltpu.SemaphoreType.DMA((steps + z_size,)),
+            pltpu.SemaphoreType.DMA((seq,)),
+        ],
+        compiler_params=pltpu.CompilerParams(
+            collective_id=0, has_side_effects=True, vmem_limit_bytes=60 * 1024 * 1024
+        ),
+    )(prompt_length, positions.reshape(1, tokens), query_rows, key_rows, value_rows, out_weight, residual)
 
 
 def largest_block(total_rows):
@@ -62,7 +285,7 @@
     return state_out
 
 
-def on_device(query_rows, key_rows, value_rows, positions, prompt_length, out_weight, residual):
+def streamed(query_rows, key_rows, value_rows, positions, prompt_length, out_weight, residual):
     tokens_here = query_rows.shape[0]
     group_size = HEADS // KV_HEADS
     queries = query_rows.reshape(tokens_here, KV_HEADS, group_size, HEAD_DIM).transpose(1, 2, 0, 3)
@@ -92,9 +315,15 @@
     return (projected + residual.astype(jnp.float32)).astype(jnp.bfloat16)
 
 
+def on_device(seq, *arrays):
+    if seq <= UNROLLED_DEVICES:
+        return fused(seq, *arrays)
+    return streamed(*arrays)
+
+
 def solution(mesh):
     return jax.shard_map(
-        on_device,
+        functools.partial(on_device, mesh.shape["seq"]),
         mesh=mesh,
         in_specs=(
             P(("groups", "seq"), None),

time: 108 us -> 30.9 us (0.29)
  waiting for transfers between devices: 57.1 us -> 0 us
  Pallas kernels: 0 us -> 28.4 us
  between operations: 14.8 us -> 0.66 us
  blocking collectives: 13.8 us -> 0 us
  matrix products: 10.4 us -> 0 us
  local copies, waits for them, and re-layouts: 9.31 us -> 1.67 us
  other arithmetic: 1.79 us -> 0 us
    all_gather x2 -> x0, waiting for transfers between devices: 55.7 us -> none  [the longest x1 33 us: on_device(): lax.all_gather(value_rows, 'seq', axis=0, tiled=True)]
    pallas_call x0 -> x1, Pallas kernels: none -> 28.4 us  [fused(): pl.pallas_call(functools.partial(fused_kernel, seq, x_size, z_size, kv_he...]
    unnamed x1 -> x0, blocking collectives: 13.8 us -> none
    dot_general x3 -> x0, matrix products: 10.4 us -> none  [the longest x1 5.66 us: on_device(): jnp.dot(attended, out_weight, preferred_element_type=jnp.float32)]
    all_gather x2 -> x0, local copies, waits for them, and re-layouts: 2.96 us -> none  [the longest x1 1.48 us: on_device(): lax.all_gather(key_rows, 'seq', axis=0, tiled=True)]
    unnamed x7 -> x1, local copies, waits for them, and re-layouts: 4.04 us -> 1.67 us
    reduce_sum x1 -> x0, other arithmetic: 1.53 us -> none  [attend_block(): totals = totals * rescale + jnp.sum(weights, axis=-1)]
    unnamed x2 -> x0, waiting for transfers between devices: 1.41 us -> none
  transfers between devices with their start and end apart: 2 -> 0, of which waited for: 2 -> 0; matrix products, arithmetic and copies ran while one was open for 8% -> 0% of each run, Pallas kernels for 0% -> 0%
where the time goes in v1:
time: 30.9 us; the launch traced here: 30.8 us
  Pallas kernels  28.4 us (92%)
  local copies, waits for them, and re-layouts  1.67 us (5%)
  between operations  0.66 us (2%)
    pallas_call x1, Pallas kernels, fused(): pl.pallas_call(functools.partial(fused_kernel, seq, x_size, z_size, kv_he...  28.4 us
    unnamed x1, local copies, waits for them, and re-layouts  1.67 us

profile of v1, /device:TPU:0, one launch (start us, length us, event | category | flops | bytes accessed | tf_op | source)
XLA Modules:
  0.0 30.8 jit_solution(2593346312870796154)
XLA Ops:
  0.7 28.4 %shard_map.73 = bf16[64,2048]{1,0:T(8,128)(2,1)} custom-call(s32[1]{0:T(128)S(6)} %copy.9.limit_ref, s32[1,64]{1,0:T(1,128)} %bitcast.1, bf16[64,2048]{1,0:T(8,128)(2,1)} %query_hbm.1, bf16[64,512]{1,0:T(8,128)(2,1)} %key_hbm.1, bf16[64,512]{1,0:T(8,128)(2,1)} %value_hbm.1, bf16[2048,2048]{1,0:T(8,128)(2,1)} %weight_hbm.1, bf16[64,2048]{1,0:T(8,128)(2,1)} %residual_hbm.1), custom_call_target="tpu_custom_call" | custom-call | tf_op jit(solution)/shard_map/pallas_call | solution.py:207
  29.1 1.7 %copy.10 = bf16[64,2048]{1,0:T(8,128)(2,1)} copy(bf16[64,2048]{1,0:T(8,128)(2,1)} %shard_map.73) | data formatting | bytes 524288

commit v2 on v1

--- a/solution.py
+++ b/solution.py
@@ -11,7 +11,6 @@
 HEAD_DIM = 128
 HEADS = 16
 KV_HEADS = 4
-UNROLLED_DEVICES = 32
 
 
 def split_chips(seq):
@@ -45,6 +44,12 @@
     x_ids = [lax.rem(x_at + d, x_size) for d in range(1, x_size)]
     x_peers = [index_of(z_at, x, core) for x in x_ids]
     other = index_of(z_at, x_at, 1 - core)
+    z_near = z_at + 1 - 2 * lax.rem(z_at, 2)
+    z_far = [lax.rem(z + 2, 4) for z in (z_at, z_near)]
+    near = index_of(z_near, x_at, core)
+    z_rest = [index_of(z, x_at, core) for z in z_far]
+    x_peer = x_peers[0]
+    x_rest = [index_of(z, 1 - x_at, core) for z in (z_near, *z_far)]
     peers = z_peers + x_peers + [other]
 
     local = []
@@ -129,17 +134,21 @@
         for peer in z_peers + x_peers + [other]:
             send(g, me, peer)
 
+    def relay(g, slot, *to):
+        arrive(g, slot)
+        for peer in to:
+            send(g, slot, peer)
+
     def forward_z(g):
-        for slot in z_slots:
-            arrive(g, slot)
-            for peer in x_peers:
-                send(g, slot, peer)
-            send(g, slot, other)
+        swap = g % 2 == 1
+        relay(g, x_peer, *((near, other) if swap else (other,)))
+        relay(g, near, *((other,) if swap else (x_peer, other)))
+        for slot in z_rest:
+            relay(g, slot, x_peer, other)
 
     def forward_x(g):
-        for slot in x_slots:
-            arrive(g, slot)
-            send(g, slot, other)
+        for slot in x_rest:
+            relay(g, slot, other)
 
     def receive(g):
         for slot in d_slots:
@@ -182,19 +191,19 @@
         else:
             out_ref[...] = (acc[...] + part).astype(jnp.bfloat16)
 
-    forward_z(0)
-    load_q.wait()
-    for g in range(kv_heads):
-        if g + 1 < kv_heads:
-            forward_z(g + 1)
-        forward_x(g)
+    def finish(g):
         receive(g)
         if g == 0:
+            load_q.wait()
             make_bias()
         if g == kv_heads - 1:
             for copy in sends:
                 copy.wait_send()
         compute(g)
+
+    stages = {"z": forward_z, "x": forward_x, "c": finish}
+    for step in 'z0 z1 x0 z2 x1 c0 z3 x2 c1 x3 c2 c3'.split():
+        stages[step[0]](int(step[1:]))
 
 
 def fused(seq, query_rows, key_rows, value_rows, positions, prompt_length, out_weight, residual):
@@ -206,9 +215,9 @@
     vmem = pl.BlockSpec(memory_space=pltpu.VMEM)
     return pl.pallas_call(
         functools.partial(fused_kernel, seq, x_size, z_size, kv_heads),
-        out_shape=jax.ShapeDtypeStruct(residual.shape, jnp.bfloat16),
+        out_shape=pltpu.VMEM(residual.shape, jnp.bfloat16),
         in_specs=[pl.BlockSpec(memory_space=pltpu.SMEM), vmem, hbm, hbm, hbm, hbm, hbm],
-        out_specs=vmem,
+        out_specs=pl.BlockSpec(memory_space=pltpu.VMEM),
         scratch_shapes=[
             pltpu.VMEM((kv_heads, seq, 2, tokens, HEAD_DIM), jnp.bfloat16),
             pltpu.VMEM((seq, 1, tokens), jnp.int32),
@@ -316,7 +325,7 @@
 
 
 def on_device(seq, *arrays):
-    if seq <= UNROLLED_DEVICES:
+    if split_chips(seq) == (2, 4):
         return fused(seq, *arrays)
     return streamed(*arrays)
 

time: 30.9 us -> 28.3 us (0.916)
  Pallas kernels: 28.4 us -> 26.8 us
  local copies, waits for them, and re-layouts: 1.67 us -> 0.71 us
    pallas_call x1, Pallas kernels: 28.4 us -> 26.8 us  [fused(): pl.pallas_call(functools.partial(fused_kernel, seq, x_size, z_size, kv_he...]
    unnamed x1, local copies, waits for them, and re-layouts: 1.67 us -> 0.71 us
where the time goes in v2:
time: 28.3 us; the launch traced here: 28.2 us
  Pallas kernels  26.8 us (95%)
  local copies, waits for them, and re-layouts  0.71 us (3%)
  between operations  0.66 us (2%)
    pallas_call x1, Pallas kernels, fused(): pl.pallas_call(functools.partial(fused_kernel, seq, x_size, z_size, kv_he...  26.8 us
    unnamed x1, local copies, waits for them, and re-layouts  0.71 us

profile of v2, /device:TPU:0, one launch (start us, length us, event | category | flops | bytes accessed | tf_op | source)
XLA Modules:
  0.0 28.2 jit_solution(1254686014408377537)
XLA Ops:
  0.7 26.8 %shard_map.73 = bf16[64,2048]{1,0:T(8,128)(2,1)S(1)} custom-call(s32[1]{0:T(128)S(6)} %copy.10.limit_ref, s32[1,64]{1,0:T(1,128)} %bitcast.1, bf16[64,2048]{1,0:T(8,128)(2,1)} %query_hbm.1, bf16[64,512]{1,0:T(8,128)(2,1)} %key_hbm.1, bf16[64,512]{1,0:T(8,128)(2,1)} %value_hbm.1, bf16[2048,2048]{1,0:T(8,128)(2,1)} %weight_hbm.1, bf16[64,2048]{1,0:T(8,128)(2,1)} %residual_hbm.1), custom_call_target="tpu_custom_call" | custom-call | tf_op jit(solution)/shard_map/pallas_call | solution.py:216
  27.5 0.7 %copy.9 = bf16[64,2048]{1,0:T(8,128)(2,1)} copy(bf16[64,2048]{1,0:T(8,128)(2,1)S(1)} %shard_map.73) | data formatting | bytes 524288
